TPU v7x, 128 devices: a whole 4x4x4 slice. The times are simulated.
128 devices in a mesh: ex: 4 (over y), ft: 32 (over x, z, core).
Axes of the slice: x: 4, y: 4, z: 4, core: 2. Of those that a mesh axis runs over, the one named last changes fastest.
Arguments:
- features: bfloat16 [2048, 262144], P(('ex', 'ft')), may hold values from -0.046875 to 0.046875
- labels: int32 [2048], P(('ex', 'ft')), may hold values 0 or 1
- start_weights: float32 [262144], P(('ex', 'ft')), may hold values from -6 to 6
- hist_s: float32 [20, 262144], P(None, ('ex', 'ft')), may hold values from -12 to 12
- hist_y: float32 [20, 262144], P(None, ('ex', 'ft')), may hold values from -30 to 30, as said below
Outputs:
- new_weights: float32 [262144], P(('ex', 'ft'))
- direction: float32 [262144], P(('ex', 'ft'))
Inputs may be any that keep to these rules, and one draw needn't show every extreme that they name: Entry by entry, hist_y times hist_s is nonnegative, and every pair has a positive inner product; every entry of hist_y is at most 1.2 times the matching entry of hist_s in magnitude.
All inputs are finite; a program needn't handle non-finite values. No bound on the sum of `labels` on one device may be relied on, other than what follows from the above.
Results may differ from a plain program's by a relative error of at most 0.0081.
Values may be sent and summed in bfloat16 or wider, within the bound.
A program may use at most 64 MiB of HBM per device.

v0:
```python
import functools

import jax
import jax.numpy as jnp
from jax import lax
from jax.experimental import pallas as pl
from jax.experimental.pallas import tpu as pltpu
from jax.sharding import PartitionSpec as P

ITERS = 2
MESH = pl.DeviceIdType.MESH
HI = lax.Precision.HIGHEST
F32 = jnp.float32
BF16 = jnp.bfloat16


def contract_last(a, b):
    return lax.dot_general(a, b, (((1,), (1,)), ((), ())), precision=HI, preferred_element_type=F32)


def kernel(
    sizes, x_hbm, lab_ref, w_ref, s_hbm, y_hbm, wout_ref, dout_ref,
    x_v, s_v, y_v, wg, rs_send, rs_recv, ar, gl, gtmp, gcore, gax,
    lab_send, lab_recv, m_send, m_recv, r_ref, acc_ref, t_ref, g_ref, gp_ref, d_ref,
    x_sem, xr_send, xr_recv, h_sem, ag_send, ag_recv, rs_ssem, rs_rsem,
    ar_ssem, ar_rsem, g_ssem, g_rsem, l_sem, m_ssem, m_rsem,
):
    ny, nx, nz = sizes
    plane = nx * nz
    chips = ny * plane
    m = s_v.shape[0]
    ex = lax.axis_index("ex")
    ft = lax.axis_index("ft")
    core = lax.rem(ft, 2)
    xz = ft // 2
    px, pz = xz // nz, lax.rem(xz, nz)
    chip = ex * plane + xz
    me = chip * 2 + core
    other = 1 - core

    def peer(oy, ox, oz):
        cy = lax.rem(ex + oy, ny)
        cx = lax.rem(px + ox, nx)
        cz = lax.rem(pz + oz, nz)
        return cy, cx * nz + cz

    hist = [
        pltpu.make_async_copy(s_hbm, s_v, h_sem.at[0]),
        pltpu.make_async_copy(y_hbm, y_v, h_sem.at[1]),
    ]
    for copy in hist:
        copy.start()
    local = []
    for h in range(2):
        copy = pltpu.make_async_copy(x_hbm.at[h, :, core], x_v.at[:, core * 2 + h], x_sem.at[h])
        copy.start()
        local.append(copy)

    barrier = pltpu.get_barrier_semaphore()

    def greet(k, carry):
        oy, ox, oz = k // plane, lax.rem(k // nz, nx), lax.rem(k, nz)
        cy, cxz = peer(oy, ox, oz)
        pl.semaphore_signal(barrier, inc=1, device_id=(cy, cxz * 2 + core), device_id_type=MESH)
        return carry

    pl.semaphore_signal(barrier, inc=1, device_id=(ex, xz * 2 + other), device_id_type=MESH)
    lax.fori_loop(1, chips, greet, 0)

    row8 = lax.broadcasted_iota(jnp.int32, (8, 128), 0)
    lane8 = lax.rem(lax.broadcasted_iota(jnp.int32, (8, 128), 1), 8)
    lab = jnp.zeros((8, 128), F32)
    for h in range(2):
        for e in range(8):
            value = lab_ref[h * 8 + e].astype(F32)
            lab = jnp.where((row8 == core * 2 + h) & (lane8 == e), value, lab)
    lab_send[...] = lab
    wg[0, chip] = w_ref[...].astype(BF16)
    acc_ref[...] = jnp.zeros_like(acc_ref)
    t_ref[...] = jnp.zeros_like(t_ref)
    gl[...] = jnp.zeros_like(gl)
    m_send[...] = jnp.zeros_like(m_send)
    gtmp[...] = jnp.zeros_like(gtmp)
    pl.semaphore_wait(barrier, chips)

    def gather_copy(it, cy, cxz):
        return pltpu.make_async_remote_copy(
            src_ref=wg.at[it, chip], dst_ref=wg.at[it, chip],
            send_sem=ag_send.at[it], recv_sem=ag_recv.at[it],
            device_id=(cy, cxz * 2 + core), device_id_type=MESH)

    def loop_far(fn):
        def body(k, carry):
            oy = far_off(k // plane, ny)
            ox = far_off(lax.rem(k // nz, nx), nx)
            oz = far_off(lax.rem(k, nz), nz)
            fn(oy, ox, oz)
            return carry
        lax.fori_loop(0, chips - 1, body, 0)

    def far_off(digit, n):
        if n == 4:
            half = digit // 2
            return (digit + 2) * (1 - half) + (3 - digit) * half
        return n - 1 - digit

    def gather_start(it):
        def fn(oy, ox, oz):
            cy, cxz = peer(oy, ox, oz)
            gather_copy(it, cy, cxz).start()
        loop_far(fn)

    def whole(ref, sem):
        return pltpu.make_async_copy(ref, ref, sem)

    gather_start(0)

    remote = []
    for h in range(2):
        copy = pltpu.make_async_remote_copy(
            src_ref=x_hbm.at[h, :, other], dst_ref=x_v.at[:, core * 2 + h],
            send_sem=xr_send.at[h], recv_sem=xr_recv.at[h],
            device_id=(ex, xz * 2 + other), device_id_type=MESH)
        copy.start()
        remote.append(copy)
    lab_copy = pltpu.make_async_remote_copy(
        src_ref=lab_send, dst_ref=lab_recv, send_sem=l_sem.at[0], recv_sem=l_sem.at[1],
        device_id=(ex, xz * 2 + other), device_id_type=MESH)
    lab_copy.start()

    for copy in hist:
        copy.wait()
    gl[0:m, 0:m] = contract_last(s_v[...], y_v[...])
    gtmp[0:m, 0:m] = contract_last(y_v[...], y_v[...])

    def gram_send(stage):
        copies = []
        if stage == 0:
            copies.append(pltpu.make_async_remote_copy(
                src_ref=gcore.at[core], dst_ref=gcore.at[core],
                send_sem=g_ssem.at[0, 0], recv_sem=g_rsem.at[0, 0],
                device_id=(ex, xz * 2 + other), device_id_type=MESH))
        else:
            n = (ny, nx, nz)[stage - 1]
            mine = (ex, px, pz)[stage - 1]
            for off in range(1, n):
                offs = [0, 0, 0]
                offs[stage - 1] = off
                cy, cxz = peer(*offs)
                copies.append(pltpu.make_async_remote_copy(
                    src_ref=gax.at[stage - 1, mine], dst_ref=gax.at[stage - 1, mine],
                    send_sem=g_ssem.at[stage, off - 1], recv_sem=g_rsem.at[stage, off - 1],
                    device_id=(cy, cxz * 2 + core), device_id_type=MESH))
        for copy in copies:
            copy.start()
        return copies

    def gram_sum(stage):
        if stage == 0:
            return gcore[0] + gcore[1]
        n = (ny, nx, nz)[stage - 1]
        total = gax[stage - 1, 0]
        for index in range(1, n):
            total = total + gax[stage - 1, index]
        return total

    gcore[core] = gl[...] + pltpu.roll(gtmp[...], 64, 1)
    gram = gram_send(0)
    gathered = chips - 1
    for copy in gram:
        copy.wait()
    gax[0, ex] = gram_sum(0)
    gram = gram_send(1)
    lab_copy.wait()

    def margins(it):
        group = min(8, chips)

        def body(k, acc):
            for j in range(group):
                c = k * group + j
                xs = x_v[c].reshape(512, 128)
                acc = acc + lax.dot_general(
                    wg[it, c], xs, (((1,), (1,)), ((), ())), preferred_element_type=F32)
            return acc
        return lax.fori_loop(0, chips // group, body, jnp.zeros((16, 512), F32))

    row16 = lax.broadcasted_iota(jnp.int32, (16, 128), 0)
    tile16 = lax.broadcasted_iota(jnp.int32, (16, 128), 1) // 8
    on_diag = row16 == tile16
    row24 = lax.broadcasted_iota(jnp.int32, (24, 128), 0)
    lane24 = lax.broadcasted_iota(jnp.int32, (24, 128), 1)
    lane1 = lax.broadcasted_iota(jnp.int32, (1, 128), 1)
    eye = jnp.where((row24 == lane24) & (row24 < m), 1.0, 0.0).astype(F32)

    weights = w_ref[...]
    rinv = rinvt = yy = diag = gamma0 = None
    for it in range(ITERS):
        whole(wg.at[it, pl.ds(0, gathered)], ag_recv.at[it]).wait()
        if it == 0:
            for copy in local:
                copy.wait()
            for copy in remote:
                copy.wait_recv()
        acc = margins(it)
        for k in range(4):
            part = jnp.where(on_diag, acc[:, k * 128:(k + 1) * 128], 0.0)
            m_send[it, k:k + 1, :] = jnp.sum(part, axis=0, keepdims=True)
        part = m_send[it]
        for shift in (8, 16, 32, 64):
            part = part + pltpu.roll(part, shift, 1)
        m_send[it] = part
        m_copy = pltpu.make_async_remote_copy(
            src_ref=m_send.at[it], dst_ref=m_recv.at[it],
            send_sem=m_ssem.at[it], recv_sem=m_rsem.at[it],
            device_id=(ex, xz * 2 + other), device_id_type=MESH)
        m_copy.start()
        if it == 0:
            for copy in gram:
                copy.wait()
            gax[1, px] = gram_sum(1)
            gram = gram_send(2)
        m_copy.wait()
        margin = m_send[it] + m_recv[it]
        resid = jax.nn.sigmoid(margin) - (lab_send[...] + lab_recv[...])
        for k in range(4):
            spread = jnp.where(on_diag, jnp.broadcast_to(resid[k:k + 1, :], (16, 128)), 0.0)
            r_ref[:, k * 128:(k + 1) * 128] = spread.astype(BF16)

        def scatter_copy(cy, cxz):
            c = cy * plane + cxz
            return pltpu.make_async_remote_copy(
                src_ref=rs_send.at[it, c], dst_ref=rs_recv.at[it, chip],
                send_sem=rs_ssem.at[it], recv_sem=rs_rsem.at[it],
                device_id=(cy, cxz * 2 + core), device_id_type=MESH)

        def scatter(k, carry):
            oy = far_off(k, ny)
            places = []
            for j in range(plane):
                ox, oz = far_off(j // nz, nx), far_off(j % nz, nz)
                cy, cxz = peer(oy, ox, oz)
                places.append((cy, cxz))
                c = cy * plane + cxz
                term = jnp.dot(r_ref[...], x_v[c].reshape(512, 128), preferred_element_type=F32)
                rs_send[it, c] = term.astype(BF16)
            for j, (cy, cxz) in enumerate(places):
                if j < plane - 1:
                    scatter_copy(cy, cxz).start()
                else:
                    @pl.when(k < ny - 1)
                    def _():
                        scatter_copy(cy, cxz).start()
            return carry

        lax.fori_loop(0, ny, scatter, 0)
        rs_recv[it, chip] = rs_send[it, chip]
        if it == 0:
            for copy in gram:
                copy.wait()
            gax[2, pz] = gram_sum(2)
            gram = gram_send(3)
            for copy in gram:
                copy.wait()
            total = gram_sum(3)
            upper = jnp.where((row24 <= lane24) & (lane24 < m), total, 0.0)
            yy = jnp.where((lane24 < m) & (row24 < m), pltpu.roll(total, 64, 1), 0.0)
            diag = upper * eye
            inv = eye
            for i in reversed(range(m)):
                line = inv[i:i + 1, :] / upper[i:i + 1, i:i + 1]
                column = jnp.where(row24[:, 0:1] < i, upper[:, i:i + 1], 0.0)
                inv = jnp.where(row24 == i, line, inv - column * line)
            rinv = inv
            t_ref[0:24, :] = inv
            rinvt = t_ref[...].T[0:24, :]
            gamma0 = upper[m - 1:m, m - 1:m] / yy[m - 1:m, m - 1:m]
        whole(rs_recv.at[it, pl.ds(0, gathered)], rs_rsem.at[it]).wait()

        def add(k, total):
            return total + rs_recv[it, k].astype(F32)
        grad = lax.fori_loop(0, chips, add, jnp.zeros((16, 128), F32), unroll=8) + 0.1 * weights
        g_ref[...] = grad
        vectors = [g_ref]
        if it > 0:
            gp_ref[...] = grad - gp_ref[...]
            vectors.append(gp_ref)
            for t in range(16):
                y_v[0:1, t * 128:(t + 1) * 128] = gp_ref[t:t + 1, :]
        for v, vec in enumerate(vectors):
            acc_s = jnp.zeros((m, 128), F32)
            acc_y = jnp.zeros((m, 128), F32)
            for t in range(16):
                line = vec[t:t + 1, :]
                acc_s = acc_s + s_v[:, t * 128:(t + 1) * 128] * line
                acc_y = acc_y + y_v[:, t * 128:(t + 1) * 128] * line
            acc_ref[v * 64:v * 64 + m, :] = acc_s
            acc_ref[v * 64 + 32:v * 64 + 32 + m, :] = acc_y
        sums = contract_last(jnp.ones((8, 128), F32), acc_ref[...])
        ar[it, me] = sums[0:1, :]

        def total_copy(cy, cxz, co):
            return pltpu.make_async_remote_copy(
                src_ref=ar.at[it, me], dst_ref=ar.at[it, me],
                send_sem=ar_ssem.at[it], recv_sem=ar_rsem.at[it],
                device_id=(cy, cxz * 2 + co), device_id_type=MESH)

        def to_both(oy, ox, oz):
            cy, cxz = peer(oy, ox, oz)
            total_copy(cy, cxz, core).start()
            total_copy(cy, cxz, other).start()
        loop_far(to_both)
        total_copy(ex, xz, other).start()
        whole(ar.at[it, pl.ds(0, 2 * chips - 1)], ar_rsem.at[it]).wait()
        tot = jnp.broadcast_to(jnp.sum(ar[it], axis=0), (8, 128))
        u, hh = tot[0:1], pltpu.roll(tot, 96, 1)[0:1]
        if it == 0:
            gamma = gamma0
            alpha = -jnp.sum(rinv * u, axis=1, keepdims=True)
            p = gamma * (jnp.sum(yy * alpha, axis=0, keepdims=True) + hh)
            p = p + jnp.sum(diag * alpha, axis=0, keepdims=True)
            coef = jnp.sum(rinvt * p, axis=1, keepdims=True)
        else:
            v, z = pltpu.roll(tot, 64, 1)[0:1], pltpu.roll(tot, 32, 1)[0:1]
            v0, z0 = v[:, 0:1], z[:, 0:1]
            gamma = v0 / z0
            old = (row24 > 0) & (lane24 > 0)
            a0 = -u[:, 0:1] / v0
            alpha = -jnp.sum(jnp.where(old, rinv, 0.0) * (u + v * a0), axis=1, keepdims=True)
            alpha = jnp.where(row24[:, 0:1] == 0, a0, alpha)
            along = jnp.sum(eye * alpha, axis=0, keepdims=True)
            newest = jnp.sum(jnp.where(lane1 < m, z, 0.0) * along, axis=1, keepdims=True)
            q = jnp.sum(jnp.where(old, yy, 0.0) * alpha, axis=0, keepdims=True) + z * a0
            q = jnp.where(lane1 == 0, newest, q)
            da = jnp.where(lane1 == 0, v0 * a0, jnp.sum(diag * alpha, axis=0, keepdims=True))
            p = gamma * (q + hh) + da
            coef = jnp.sum(jnp.where(old, rinvt, 0.0) * p, axis=1, keepdims=True)
            along = jnp.sum(eye * coef, axis=0, keepdims=True)
            rest = jnp.sum(jnp.where((lane1 > 0) & (lane1 < m), v, 0.0) * along, axis=1, keepdims=True)
            c0 = (p[:, 0:1] - rest) / v0
            coef = jnp.where(row24[:, 0:1] == 0, c0, coef)
        cs, cy_ = coef[0:m], (-gamma * alpha)[0:m]
        for t in range(16):
            cols = slice(t * 128, (t + 1) * 128)
            d_ref[t:t + 1, :] = jnp.sum(cs * s_v[:, cols] + cy_ * y_v[:, cols], axis=0, keepdims=True)
        direction = d_ref[...] - gamma * g_ref[...]
        new = weights + direction
        if it < ITERS - 1:
            wg[it + 1, chip] = new.astype(BF16)
            gather_start(it + 1)
            gp_ref[...] = grad
            d_ref[...] = new - weights
            for t in range(16):
                s_v[0:1, t * 128:(t + 1) * 128] = d_ref[t:t + 1, :]
            weights = new
        else:
            wout_ref[...] = new
            dout_ref[...] = direction

    for copy in remote:
        copy.wait_send()
    for it in range(ITERS):
        whole(wg.at[it, pl.ds(0, gathered)], ag_send.at[it]).wait()
        whole(rs_send.at[it, pl.ds(0, gathered)], rs_ssem.at[it]).wait()
        whole(ar.at[it, pl.ds(0, 2 * chips - 1)], ar_ssem.at[it]).wait()


def per_device(sizes, features, labels, start_weights, hist_s, hist_y):
    ny, nx, nz = sizes
    chips = ny * nx * nz
    m = hist_s.shape[0]
    x = features.reshape(2, 8, chips, 2, 16, 128).transpose(0, 2, 3, 4, 1, 5)
    x = x.reshape(2, chips, 2, 128, 128)
    vmem = pl.BlockSpec(memory_space=pltpu.VMEM)
    hbm = pl.BlockSpec(memory_space=pl.ANY)
    dma = pltpu.SemaphoreType.DMA
    own = jax.ShapeDtypeStruct((16, 128), F32)
    new, direction = pl.pallas_call(
        functools.partial(kernel, sizes),
        out_shape=(own, own),
        in_specs=[hbm, pl.BlockSpec(memory_space=pltpu.SMEM), vmem, hbm, hbm],
        out_specs=(vmem, vmem),
        scratch_shapes=[
            pltpu.VMEM((chips, 4, 128, 128), BF16),
            pltpu.VMEM((m, 2048), F32),
            pltpu.VMEM((m, 2048), F32),
            pltpu.VMEM((ITERS, chips, 16, 128), BF16),
            pltpu.VMEM((ITERS, chips, 16, 128), BF16),
            pltpu.VMEM((ITERS, chips, 16, 128), BF16),
            pltpu.VMEM((ITERS, 2 * chips, 1, 128), F32),
            pltpu.VMEM((24, 128), F32),
            pltpu.VMEM((24, 128), F32),
            pltpu.VMEM((2, 24, 128), F32),
            pltpu.VMEM((3, 4, 24, 128), F32),
            pltpu.VMEM((8, 128), F32),
            pltpu.VMEM((8, 128), F32),
            pltpu.VMEM((ITERS, 8, 128), F32),
            pltpu.VMEM((ITERS, 8, 128), F32),
            pltpu.VMEM((16, 512), BF16),
            pltpu.VMEM((128, 128), F32),
            pltpu.VMEM((128, 128), F32),
            pltpu.VMEM((16, 128), F32),
            pltpu.VMEM((16, 128), F32),
            pltpu.VMEM((16, 128), F32),
            dma((2,)), dma((2,)), dma((2,)), dma((2,)),
            dma((ITERS,)), dma((ITERS,)), dma((ITERS,)), dma((ITERS,)),
            dma((ITERS,)), dma((ITERS,)),
            dma((4, 3)), dma((4, 3)), dma((2,)), dma((ITERS,)), dma((ITERS,)),
        ],
        compiler_params=pltpu.CompilerParams(collective_id=0, has_side_effects=True),
    )(x, labels, start_weights.reshape(16, 128), hist_s, hist_y)
    return new.reshape(2048), direction.reshape(2048)


def solution(mesh):
    ny, rest = mesh.shape["ex"], mesh.shape["ft"] // 2
    nx = round(rest ** 0.5)
    sizes = (ny, nx, rest // nx)
    return jax.shard_map(
        functools.partial(per_device, sizes),
        mesh=mesh,
        in_specs=(
            P(("ex", "ft"), None),
            P(("ex", "ft")),
            P(("ex", "ft")),
            P(None, ("ex", "ft")),
            P(None, ("ex", "ft")),
        ),
        out_specs=(P(("ex", "ft")), P(("ex", "ft"))),
        check_vma=False,
    )
```

profile of v0, /device:TPU:1, one launch (start us, length us, event | category | flops | bytes accessed | tf_op | source)
XLA Modules:
  0.0 72.4 jit_solution(13136247832691823294)
XLA Ops:
  0.6 69.1 %shard_map.68 = (f32[16,128]{1,0:T(8,128)}, f32[16,128]{1,0:T(8,128)}) custom-call(bf16[2,64,2,128,128]{4,3,2,1,0:T(8,128)(2,1)} %bitcast.8, s32[16]{0:T(128)} %lab_ref.1, f32[16,128]{1,0:T(8,128)} %bitcast.9, f32[20,2048]{1,0:T(8,128)} %s_hbm.1, f32[20,2048]{1,0:T(8,128)} %y_hbm.1), custom_call_target="tpu_custom_call" | custom-call | tf_op jit(solution)/shard_map/pallas_call | solution.py:378
  69.8 1.3 %copy.9 = f32[2048]{0:T(1024)} copy(f32[2048]{0:T(1024)} %bitcast.11) | data formatting | bytes 16384
  71.1 1.3 %copy.10 = f32[2048]{0:T(1024)} copy(f32[2048]{0:T(1024)} %bitcast.10) | data formatting | bytes 16384
where the time goes:
time: 72.7 us; the launch traced here: 72.4 us
  Pallas kernels  69.1 us (95%)
  local copies, waits for them, and re-layouts  2.59 us (4%)
    pallas_call x1, Pallas kernels, per_device(): pl.pallas_call(functools.partial(kernel, sizes), out_shape=(own, own), in...  69.1 us
    unnamed x2, local copies, waits for them, and re-layouts  2.59 us

commit v1 on v0

v1 whole, which is shorter than its diff:
```python
import functools
import itertools

import jax
import jax.numpy as jnp
from jax import lax
from jax.experimental import pallas as pl
from jax.experimental.pallas import tpu as pltpu
from jax.sharding import PartitionSpec as P

ITERS = 2
MESH = pl.DeviceIdType.MESH
HI = lax.Precision.HIGHEST
F32 = jnp.float32
BF16 = jnp.bfloat16
BATCHES = (8, 8, 16, 16, 16)


def contract_last(a, b):
    return lax.dot_general(a, b, (((1,), (1,)), ((), ())), precision=HI, preferred_element_type=F32)


def hops(offset, sizes):
    return sum(min(o, n - o) for o, n in zip(offset, sizes))


def kernel(
    sizes, x_hbm, lab_hbm, w_hbm, s_hbm, y_hbm, out_ref,
    x_v, x_out, lab_ref, w_ref, s_v, y_v, w_own, wg, rs_send, rs_recv, ar_own, ar, gl, gtmp, gcore, gax,
    lab_send, lab_recv, m_send, m_recv, r_ref, acc_ref, t_ref, g_ref, gp_ref, d_ref,
    x_sem, xr_send, xr_recv, h_sem, ag_send, ag_recv, rs_ssem, rs_rsem,
    ar_ssem, ar_rsem, g_ssem, g_rsem, l_sem, m_ssem, m_rsem,
):
    ny, nx, nz = sizes
    plane = nx * nz
    chips = ny * plane
    m = s_v.shape[0]
    ex = lax.axis_index("ex")
    ft = lax.axis_index("ft")
    core = lax.rem(ft, 2)
    xz = ft // 2
    px, pz = xz // nz, lax.rem(xz, nz)
    chip = ex * plane + xz
    other = 1 - core
    partner = (ex, xz * 2 + other)

    steps = (plane, nz, 1)
    mine = (ex, px, pz)
    ahead = [[lax.rem(p + o, n) * d for o in range(n)] for p, n, d in zip(mine, sizes, steps)]
    behind = [[lax.rem(p + n - o, n) * d for o in range(n)] for p, n, d in zip(mine, sizes, steps)]

    def index(offset, table):
        return table[0][offset[0]] + table[1][offset[1]] + table[2][offset[2]]

    at_y = [lax.rem(ex + o, ny) for o in range(ny)]

    def peer(offset):
        return at_y[offset[0]], ahead[1][offset[1]] + ahead[2][offset[2]]

    def dest(place):
        return (place[0], place[1] * 2 + other)

    offsets = sorted(
        itertools.product(*map(range, sizes)),
        key=lambda o: -hops(o, sizes))
    rounds = chips // 8

    def round_of(offset):
        j = 0
        for o, n in zip(offset, sizes):
            j = 2 * j + (1 if n == 4 and o in (3, 0) else 0)
        return {3: 4, 4: 3}.get(j, j)

    def round_blocks(k, table):
        j = k + jnp.where(k == 3, 1, 0) - jnp.where(k == 4, 1, 0)
        lows = []
        for places, high in zip(table, (j // 4, lax.rem(j // 2, 2), lax.rem(j, 2))):
            if len(places) == 4:
                lows.append([jnp.where(high == 0, places[2], places[3]), jnp.where(high == 0, places[1], places[0])])
            else:
                lows.append([places[1], places[0]])
        return [a + b + c for a in lows[0] for b in lows[1] for c in lows[2]]

    hist = [
        pltpu.make_async_copy(s_hbm, s_v, h_sem.at[0]),
        pltpu.make_async_copy(y_hbm, y_v, h_sem.at[1]),
    ]
    small = [
        pltpu.make_async_copy(w_hbm, w_ref, h_sem.at[2]),
        pltpu.make_async_copy(lab_hbm, lab_ref, h_sem.at[3]),
    ]
    for copy in small + hist:
        copy.start()
    local = []
    for h in range(2):
        copy = pltpu.make_async_copy(x_hbm.at[h, :, other], x_v.at[:, h], x_sem.at[h])
        copy.start()
        local.append(copy)
    staged = []
    for h in range(2):
        copy = pltpu.make_async_copy(x_hbm.at[h, :, core], x_out.at[:, h], x_sem.at[2 + h])
        copy.start()
        staged.append(copy)

    barrier = pltpu.get_barrier_semaphore()
    for offset in offsets:
        pl.semaphore_signal(barrier, inc=1, device_id=dest(peer(offset)), device_id_type=MESH)

    row8 = lax.broadcasted_iota(jnp.int32, (8, 128), 0)
    lanes8 = lax.broadcasted_iota(jnp.int32, (8, 128), 1)
    for copy in small:
        copy.wait()
    lab = jnp.zeros((8, 128), F32)
    for h in range(2):
        for e in range(8):
            value = lab_ref[h * 8 + e].astype(F32)
            lab = jnp.where((row8 == e) & (lanes8 // 32 == h), value, lab)
    lab_send[...] = lab
    w_own[0] = w_ref[...].astype(BF16)
    acc_ref[...] = jnp.zeros_like(acc_ref)
    t_ref[...] = jnp.zeros_like(t_ref)
    gl[...] = jnp.zeros_like(gl)
    gtmp[...] = jnp.zeros_like(gtmp)
    for copy in hist:
        copy.wait()
    gl[0:m, 0:m] = contract_last(s_v[...], y_v[...])
    gtmp[0:m, 0:m] = contract_last(y_v[...], y_v[...])
    gcore[core] = gl[...] + pltpu.roll(gtmp[...], 64, 1)
    pl.semaphore_wait(barrier, chips)

    def whole(ref, sem):
        return pltpu.make_async_copy(ref, ref, sem)

    def gather_start(it):
        for offset in offsets:
            pltpu.make_async_remote_copy(
                src_ref=w_own.at[it], dst_ref=wg.at[it, chip],
                send_sem=ag_send.at[it], recv_sem=ag_recv.at[it, round_of(offset)],
                device_id=dest(peer(offset)), device_id_type=MESH).start()

    gather_start(0)

    def gram_send(stage):
        copies = []
        if stage == 3:
            copies.append(pltpu.make_async_remote_copy(
                src_ref=gcore.at[core], dst_ref=gcore.at[core],
                send_sem=g_ssem.at[3, 0], recv_sem=g_rsem.at[3, 0],
                device_id=partner, device_id_type=MESH))
        else:
            own = mine[stage]
            for off in range(1, sizes[stage]):
                offset = tuple(off if a == stage else 0 for a in range(3))
                copies.append(pltpu.make_async_remote_copy(
                    src_ref=gax.at[stage, own], dst_ref=gax.at[stage, own],
                    send_sem=g_ssem.at[stage, off - 1], recv_sem=g_rsem.at[stage, off - 1],
                    device_id=dest(peer(offset)), device_id_type=MESH))
        for copy in copies:
            copy.start()
        return copies

    def gram_sum(stage, copies):
        for copy in copies:
            copy.wait()
        if stage == 3:
            return gcore[0] + gcore[1]
        total = gax[stage, 0]
        for place in range(1, sizes[stage]):
            total = total + gax[stage, place]
        return total

    gram = gram_send(3)
    for copy in staged:
        copy.wait()
    for offset in reversed(offsets):
        c = index(offset, behind)
        pltpu.make_async_remote_copy(
            src_ref=x_out.at[c], dst_ref=x_v.at[c, 2:4],
            send_sem=xr_send.at[0], recv_sem=xr_recv.at[round_of(offset)],
            device_id=partner, device_id_type=MESH).start()
    lab_copy = pltpu.make_async_remote_copy(
        src_ref=lab_send, dst_ref=lab_recv, send_sem=l_sem.at[0], recv_sem=l_sem.at[1],
        device_id=partner, device_id_type=MESH)
    lab_copy.start()

    gax[0, ex] = gram_sum(3, gram)
    gram = gram_send(0)

    row16 = lax.broadcasted_iota(jnp.int32, (16, 128), 0)
    tile16 = lax.broadcasted_iota(jnp.int32, (16, 128), 1) // 8
    on_diag = row16 == tile16
    row24 = lax.broadcasted_iota(jnp.int32, (24, 128), 0)
    lane24 = lax.broadcasted_iota(jnp.int32, (24, 128), 1)
    lane1 = lax.broadcasted_iota(jnp.int32, (1, 128), 1)
    eye = jnp.where((row24 == lane24) & (row24 < m), 1.0, 0.0).astype(F32)
    turn = jnp.where(lax.rem(lanes8, 8) == row8, 1.0, 0.0).astype(F32)

    def margin_terms(it, blocks, accs):
        accs = list(accs)
        left = jnp.concatenate([wg[it, c] for c in blocks], axis=1)
        right = jnp.concatenate([x_v[c, 3] for c in blocks], axis=1)
        accs[6] = accs[6] + lax.dot_general(
            left, right, (((1,), (1,)), ((), ())), preferred_element_type=F32)
        for c in blocks:
            for t in range(0, 16, 2):
                w = wg[it, c, t:t + 2, :].astype(F32)
                w = jnp.concatenate(
                    [jnp.broadcast_to(w[0:1], (8, 128)), jnp.broadcast_to(w[1:2], (8, 128))], axis=0)
                for f in range(3):
                    prod = x_v[c, f, t * 8:t * 8 + 16, :].astype(F32) * w
                    accs[f] = accs[f] + prod[0:8]
                    accs[3 + f] = accs[3 + f] + prod[8:16]
        return tuple(accs)

    def zeros(count):
        return tuple(jnp.zeros((8, 128), F32) for _ in range(count))

    def lane_sums(accs):
        return [jnp.sum(acc, axis=1, keepdims=True) for acc in accs]

    def spread_halves(cols):
        out = jnp.broadcast_to(cols[0], (8, 128))
        for k in range(1, 4):
            out = jnp.where(lanes8 // 32 == k, cols[k], out)
        return out

    weights = w_ref[...]
    rinv = rinvt = yy = diag = gamma0 = None
    for it in range(ITERS):
        if it == 0:
            for copy in local:
                copy.wait()

        def arrive(i, accs):
            k = rounds - 1 - i
            if it == 0:
                whole(x_out.at[pl.ds(0, 8)], xr_recv.at[k]).wait()
            whole(wg.at[it, pl.ds(0, 8)], ag_recv.at[it, k]).wait()
            return margin_terms(it, round_blocks(k, behind), accs)

        accs = lax.fori_loop(0, rounds, arrive, zeros(6) + (jnp.zeros((16, 128), F32),))
        line = jnp.sum(jnp.where(on_diag, accs[6], 0.0), axis=0, keepdims=True)
        cols = lane_sums([accs[f] + accs[3 + f] for f in range(3)] + [turn * line])
        m_send[it] = spread_halves(cols)
        m_copy = pltpu.make_async_remote_copy(
            src_ref=m_send.at[it], dst_ref=m_recv.at[it],
            send_sem=m_ssem.at[it], recv_sem=m_rsem.at[it],
            device_id=partner, device_id_type=MESH)
        m_copy.start()
        if it == 0:
            lab_copy.wait()
            lab_all = lab_send[...] + pltpu.roll(lab_recv[...], 64, 1)
            gax[1, px] = gram_sum(0, gram)
            gram = gram_send(1)
        m_copy.wait()
        margin = m_send[it] + pltpu.roll(m_recv[it], 64, 1)
        resid = jax.nn.sigmoid(margin) - lab_all
        for k in range(4):
            line = jnp.sum(turn * resid[:, k * 32:k * 32 + 1], axis=0, keepdims=True)
            r_ref[:, k * 128:(k + 1) * 128] = jnp.where(on_diag, line, 0.0).astype(BF16)

        def scatter_send(batch):
            for offset in batch:
                pltpu.make_async_remote_copy(
                    src_ref=rs_send.at[it, index(offset, ahead)], dst_ref=rs_recv.at[it, chip],
                    send_sem=rs_ssem.at[it], recv_sem=rs_rsem.at[it],
                    device_id=dest(peer(offset)), device_id_type=MESH).start()

        lines = r_ref[...]
        start = 0
        for size in BATCHES:
            batch = offsets[start:min(start + size, chips)]
            start += size
            for j in range(0, len(batch), 2):
                c0, c1 = index(batch[j], ahead), index(batch[j + 1], ahead)
                both = jnp.concatenate([x_v[c0].reshape(512, 128), x_v[c1].reshape(512, 128)], axis=1)
                term = jnp.dot(lines, both, preferred_element_type=F32).astype(BF16)
                rs_send[it, c0] = term[:, 0:128]
                rs_send[it, c1] = term[:, 128:256]
            scatter_send(batch)
        if it == 0:
            gax[2, pz] = gram_sum(1, gram)
            gram = gram_send(2)
            total = gram_sum(2, gram)
            upper = jnp.where((row24 <= lane24) & (lane24 < m), total, 0.0)
            yy = jnp.where((lane24 < m) & (row24 < m), pltpu.roll(total, 64, 1), 0.0)
            diag = upper * eye
            inv = eye
            for i in reversed(range(m)):
                line = inv[i:i + 1, :] / upper[i:i + 1, i:i + 1]
                column = jnp.where(row24[:, 0:1] < i, upper[:, i:i + 1], 0.0)
                inv = jnp.where(row24 == i, line, inv - column * line)
            rinv = inv
            t_ref[0:24, :] = inv
            rinvt = t_ref[...].T[0:24, :]
            gamma0 = upper[m - 1:m, m - 1:m] / yy[m - 1:m, m - 1:m]
        whole(rs_recv.at[it], rs_rsem.at[it]).wait()

        def add(k, total):
            return total + rs_recv[it, k].astype(F32)
        grad = lax.fori_loop(0, chips, add, jnp.zeros((16, 128), F32), unroll=8) + 0.1 * weights
        g_ref[...] = grad
        vectors = [g_ref]
        if it > 0:
            gp_ref[...] = grad - gp_ref[...]
            vectors.append(gp_ref)
            for t in range(16):
                y_v[0:1, t * 128:(t + 1) * 128] = gp_ref[t:t + 1, :]
        for v, vec in enumerate(vectors):
            acc_s = jnp.zeros((m, 128), F32)
            acc_y = jnp.zeros((m, 128), F32)
            for t in range(16):
                line = vec[t:t + 1, :]
                acc_s = acc_s + s_v[:, t * 128:(t + 1) * 128] * line
                acc_y = acc_y + y_v[:, t * 128:(t + 1) * 128] * line
            acc_ref[v * 64:v * 64 + m, :] = acc_s
            acc_ref[v * 64 + 32:v * 64 + 32 + m, :] = acc_y
        sums = contract_last(jnp.ones((8, 128), F32), acc_ref[...])
        ar_own[it] = sums[0:1, :]
        ar[it, chip * 2 + core] = sums[0:1, :]

        def total_send(device):
            pltpu.make_async_remote_copy(
                src_ref=ar_own.at[it], dst_ref=ar.at[it, chip * 2 + core],
                send_sem=ar_ssem.at[it], recv_sem=ar_rsem.at[it],
                device_id=device, device_id_type=MESH).start()

        for offset in offsets[:-1]:
            cy, cxz = peer(offset)
            total_send((cy, cxz * 2))
            total_send((cy, cxz * 2 + 1))
        total_send(partner)
        whole(ar.at[it, pl.ds(0, 2 * chips - 1)], ar_rsem.at[it]).wait()
        tot = jnp.broadcast_to(jnp.sum(ar[it], axis=0), (8, 128))
        u, hh = tot[0:1], pltpu.roll(tot, 96, 1)[0:1]
        if it == 0:
            gamma = gamma0
            alpha = -jnp.sum(rinv * u, axis=1, keepdims=True)
            p = gamma * (jnp.sum(yy * alpha, axis=0, keepdims=True) + hh)
            p = p + jnp.sum(diag * alpha, axis=0, keepdims=True)
            coef = jnp.sum(rinvt * p, axis=1, keepdims=True)
        else:
            v, z = pltpu.roll(tot, 64, 1)[0:1], pltpu.roll(tot, 32, 1)[0:1]
            v0, z0, u0 = v[:, 0:1], z[:, 0:1], u[:, 0:1]
            gamma = v0 / z0
            a0 = -u0 / v0
            old = (row24 > 0) & (lane24 > 0)
            rm, rmt = jnp.where(old, rinv, 0.0), jnp.where(old, rinvt, 0.0)
            ru = jnp.sum(rm * u, axis=1, keepdims=True)
            rv = jnp.sum(rm * v, axis=1, keepdims=True)
            rv_flat = jnp.sum(eye * rv, axis=0, keepdims=True)
            alpha = jnp.where(row24[:, 0:1] == 0, a0, -(ru + rv * a0))
            flat = jnp.sum(eye * alpha, axis=0, keepdims=True)
            newest = jnp.sum(jnp.where(lane1 < m, z, 0.0) * flat, axis=1, keepdims=True)
            q = jnp.sum(jnp.where(old, yy, 0.0) * alpha, axis=0, keepdims=True) + z * a0
            p = gamma * (q + hh) + jnp.sum(diag * alpha, axis=0, keepdims=True)
            coef = jnp.sum(rmt * p, axis=1, keepdims=True)
            rest = jnp.sum(rv_flat * p, axis=1, keepdims=True)
            c0 = (gamma * (newest + hh[:, 0:1]) + v0 * a0 - rest) / v0
            coef = jnp.where(row24[:, 0:1] == 0, c0, coef)
        cs, cy = coef[0:m], (-gamma * alpha)[0:m]
        for t in range(16):
            cols = slice(t * 128, (t + 1) * 128)
            d_ref[t:t + 1, :] = jnp.sum(cs * s_v[:, cols] + cy * y_v[:, cols], axis=0, keepdims=True)
        direction = d_ref[...] - gamma * g_ref[...]
        new = weights + direction
        if it < ITERS - 1:
            w_own[it + 1] = new.astype(BF16)
            gather_start(it + 1)
            gp_ref[...] = grad
            d_ref[...] = new - weights
            for t in range(16):
                s_v[0:1, t * 128:(t + 1) * 128] = d_ref[t:t + 1, :]
            weights = new
        else:
            out_ref[0] = new
            out_ref[1] = direction

    whole(x_out, xr_send.at[0]).wait()
    for it in range(ITERS):
        whole(wg.at[it], ag_send.at[it]).wait()
        whole(rs_send.at[it], rs_ssem.at[it]).wait()
        whole(ar.at[it, pl.ds(0, 2 * chips - 1)], ar_ssem.at[it]).wait()


def per_device(sizes, features, labels, start_weights, hist_s, hist_y):
    ny, nx, nz = sizes
    chips = ny * nx * nz
    m = hist_s.shape[0]
    x = features.reshape(2, 8, chips, 2, 16, 128).transpose(0, 2, 3, 4, 1, 5)
    x = x.reshape(2, chips, 2, 128, 128)
    vmem = pl.BlockSpec(memory_space=pltpu.VMEM)
    hbm = pl.BlockSpec(memory_space=pl.ANY)
    dma = pltpu.SemaphoreType.DMA
    out = pl.pallas_call(
        functools.partial(kernel, sizes),
        out_shape=pltpu.VMEM((2, 16, 128), F32),
        in_specs=[hbm] * 5,
        out_specs=vmem,
        scratch_shapes=[
            pltpu.VMEM((chips, 4, 128, 128), BF16),
            pltpu.VMEM((chips, 2, 128, 128), BF16),
            pltpu.SMEM((16,), jnp.int32),
            pltpu.VMEM((16, 128), F32),
            pltpu.VMEM((m, 2048), F32),
            pltpu.VMEM((m, 2048), F32),
            pltpu.VMEM((ITERS, 16, 128), BF16),
            pltpu.VMEM((ITERS, chips, 16, 128), BF16),
            pltpu.VMEM((ITERS, chips, 16, 128), BF16),
            pltpu.VMEM((ITERS, chips, 16, 128), BF16),
            pltpu.VMEM((ITERS, 1, 128), F32),
            pltpu.VMEM((ITERS, 2 * chips, 1, 128), F32),
            pltpu.VMEM((24, 128), F32),
            pltpu.VMEM((24, 128), F32),
            pltpu.VMEM((2, 24, 128), F32),
            pltpu.VMEM((3, 4, 24, 128), F32),
            pltpu.VMEM((8, 128), F32),
            pltpu.VMEM((8, 128), F32),
            pltpu.VMEM((ITERS, 8, 128), F32),
            pltpu.VMEM((ITERS, 8, 128), F32),
            pltpu.VMEM((16, 512), BF16),
            pltpu.VMEM((128, 128), F32),
            pltpu.VMEM((128, 128), F32),
            pltpu.VMEM((16, 128), F32),
            pltpu.VMEM((16, 128), F32),
            pltpu.VMEM((16, 128), F32),
            dma((4,)), dma((1,)), dma((chips // 8,)), dma((4,)),
            dma((ITERS,)), dma((ITERS, chips // 8)), dma((ITERS,)), dma((ITERS,)),
            dma((ITERS,)), dma((ITERS,)),
            dma((4, 3)), dma((4, 3)), dma((2,)), dma((ITERS,)), dma((ITERS,)),
        ],
        compiler_params=pltpu.CompilerParams(collective_id=0, has_side_effects=True),
    )(x, labels, start_weights.reshape(16, 128), hist_s, hist_y)
    out = out.reshape(2, 2048)
    return out[0], out[1]


def solution(mesh):
    ny, rest = mesh.shape["ex"], mesh.shape["ft"] // 2
    nx = round(rest ** 0.5)
    sizes = (ny, nx, rest // nx)
    return jax.shard_map(
        functools.partial(per_device, sizes),
        mesh=mesh,
        in_specs=(
            P(("ex", "ft"), None),
            P(("ex", "ft")),
            P(("ex", "ft")),
            P(None, ("ex", "ft")),
            P(None, ("ex", "ft")),
        ),
        out_specs=(P(("ex", "ft")), P(("ex", "ft"))),
        check_vma=False,
    )
```

time: 72.7 us -> 57.2 us (0.79)
  Pallas kernels: 69.1 us -> 55.8 us
  local copies, waits for them, and re-layouts: 2.59 us -> 0.61 us
    pallas_call x1, Pallas kernels: 69.1 us -> 55.8 us  [per_device(): pl.pallas_call(functools.partial(kernel, sizes), out_shape=pltpu.VMEM((2,...]
    unnamed x2 -> x0, local copies, waits for them, and re-layouts: 2.59 us -> none
where the time goes in v1:
time: 57.2 us; the launch traced here: 57.1 us
  Pallas kernels  55.8 us (98%)
  between operations  0.64 us (1%)
  local copies, waits for them, and re-layouts  0.61 us (1%)
    pallas_call x1, Pallas kernels, per_device(): pl.pallas_call(functools.partial(kernel, sizes), out_shape=pltpu.VMEM((2,...  55.8 us

profile of v1, /device:TPU:1, one launch (start us, length us, event | category | flops | bytes accessed | tf_op | source)
XLA Modules:
  0.0 57.1 jit_solution(5928200266491743646)
XLA Ops:
  0.6 55.8 %shard_map.68 = f32[2,16,128]{2,1,0:T(8,128)S(1)} custom-call(bf16[2,64,2,128,128]{4,3,2,1,0:T(8,128)(2,1)} %bitcast.10, s32[16]{0:T(128)} %lab_hbm.1, f32[16,128]{1,0:T(8,128)} %bitcast.11, f32[20,2048]{1,0:T(8,128)} %s_hbm.1, f32[20,2048]{1,0:T(8,128)} %y_hbm.1), custom_call_target="tpu_custom_call" | custom-call | tf_op jit(solution)/shard_map/pallas_call | solution.py:395
  56.5 0.6 %slice_bitcast_fusion = (f32[2048]{0:T(1024)}, f32[2048]{0:T(1024)}) fusion(f32[2,16,128]{2,1,0:T(8,128)S(1)} %shard_map.68), kind=kLoop, calls=%fused_computation | loop fusion | bytes 32768 | tf_op jit(solution)/shard_map/squeeze | solution.py:435

commit v2 on v1

--- a/solution.py
+++ b/solution.py
@@ -26,8 +26,8 @@
 
 def kernel(
     sizes, x_hbm, lab_hbm, w_hbm, s_hbm, y_hbm, out_ref,
-    x_v, x_out, lab_ref, w_ref, s_v, y_v, w_own, wg, rs_send, rs_recv, ar_own, ar, gl, gtmp, gcore, gax,
-    lab_send, lab_recv, m_send, m_recv, r_ref, acc_ref, t_ref, g_ref, gp_ref, d_ref,
+    x_v, x_out, x_f, lab_ref, w_ref, s_v, y_v, w_own, wg, rs_send, rs_recv, ar_own, ar, gl, gtmp, gcore, gax,
+    lab_send, lab_recv, m_send, m_recv, r_ref, t_ref, g_ref, gp_ref, d_ref,
     x_sem, xr_send, xr_recv, h_sem, ag_send, ag_recv, rs_ssem, rs_rsem,
     ar_ssem, ar_rsem, g_ssem, g_rsem, l_sem, m_ssem, m_rsem,
 ):
@@ -114,10 +114,9 @@
     for h in range(2):
         for e in range(8):
             value = lab_ref[h * 8 + e].astype(F32)
-            lab = jnp.where((row8 == e) & (lanes8 // 32 == h), value, lab)
-    lab_send[...] = lab
+            lab = jnp.where((row8 == e), value, lab)
+        lab_send[h] = lab
     w_own[0] = w_ref[...].astype(BF16)
-    acc_ref[...] = jnp.zeros_like(acc_ref)
     t_ref[...] = jnp.zeros_like(t_ref)
     gl[...] = jnp.zeros_like(gl)
     gtmp[...] = jnp.zeros_like(gtmp)
@@ -191,25 +190,31 @@
     on_diag = row16 == tile16
     row24 = lax.broadcasted_iota(jnp.int32, (24, 128), 0)
     lane24 = lax.broadcasted_iota(jnp.int32, (24, 128), 1)
+    row_m, lane_m = row24[0:m], lane24[0:m]
     lane1 = lax.broadcasted_iota(jnp.int32, (1, 128), 1)
     eye = jnp.where((row24 == lane24) & (row24 < m), 1.0, 0.0).astype(F32)
     turn = jnp.where(lax.rem(lanes8, 8) == row8, 1.0, 0.0).astype(F32)
 
     def margin_terms(it, blocks, accs):
         accs = list(accs)
-        left = jnp.concatenate([wg[it, c] for c in blocks], axis=1)
-        right = jnp.concatenate([x_v[c, 3] for c in blocks], axis=1)
-        accs[6] = accs[6] + lax.dot_general(
-            left, right, (((1,), (1,)), ((), ())), preferred_element_type=F32)
+        count = 3 if it == 0 else 4
+        if it == 0:
+            left = jnp.concatenate([wg[it, c] for c in blocks], axis=1)
+            right = jnp.concatenate([x_v[c, 3] for c in blocks], axis=1)
+            accs[6] = accs[6] + lax.dot_general(
+                left, right, (((1,), (1,)), ((), ())), preferred_element_type=F32)
         for c in blocks:
             for t in range(0, 16, 2):
                 w = wg[it, c, t:t + 2, :].astype(F32)
                 w = jnp.concatenate(
                     [jnp.broadcast_to(w[0:1], (8, 128)), jnp.broadcast_to(w[1:2], (8, 128))], axis=0)
-                for f in range(3):
-                    prod = x_v[c, f, t * 8:t * 8 + 16, :].astype(F32) * w
+                for f in range(count):
+                    if it == 0:
+                        prod = x_v[c, f, t * 8:t * 8 + 16, :].astype(F32) * w
+                    else:
+                        prod = x_f[c, f, t * 8:t * 8 + 16, :] * w
                     accs[f] = accs[f] + prod[0:8]
-                    accs[3 + f] = accs[3 + f] + prod[8:16]
+                    accs[count + f] = accs[count + f] + prod[8:16]
         return tuple(accs)
 
     def zeros(count):
@@ -217,12 +222,6 @@
 
     def lane_sums(accs):
         return [jnp.sum(acc, axis=1, keepdims=True) for acc in accs]
-
-    def spread_halves(cols):
-        out = jnp.broadcast_to(cols[0], (8, 128))
-        for k in range(1, 4):
-            out = jnp.where(lanes8 // 32 == k, cols[k], out)
-        return out
 
     weights = w_ref[...]
     rinv = rinvt = yy = diag = gamma0 = None
@@ -238,10 +237,15 @@
             whole(wg.at[it, pl.ds(0, 8)], ag_recv.at[it, k]).wait()
             return margin_terms(it, round_blocks(k, behind), accs)
 
-        accs = lax.fori_loop(0, rounds, arrive, zeros(6) + (jnp.zeros((16, 128), F32),))
-        line = jnp.sum(jnp.where(on_diag, accs[6], 0.0), axis=0, keepdims=True)
-        cols = lane_sums([accs[f] + accs[3 + f] for f in range(3)] + [turn * line])
-        m_send[it] = spread_halves(cols)
+        if it == 0:
+            accs = lax.fori_loop(0, rounds, arrive, zeros(6) + (jnp.zeros((16, 128), F32),))
+            line = jnp.sum(jnp.where(on_diag, accs[6], 0.0), axis=0, keepdims=True)
+            cols = lane_sums([accs[f] + accs[3 + f] for f in range(3)] + [turn * line])
+        else:
+            accs = lax.fori_loop(0, rounds, arrive, zeros(8))
+            cols = lane_sums([accs[f] + accs[4 + f] for f in range(4)])
+        for k in range(4):
+            m_send[it, (k + 2) % 4] = jnp.broadcast_to(cols[k], (8, 128))
         m_copy = pltpu.make_async_remote_copy(
             src_ref=m_send.at[it], dst_ref=m_recv.at[it],
             send_sem=m_ssem.at[it], recv_sem=m_rsem.at[it],
@@ -249,14 +253,13 @@
         m_copy.start()
         if it == 0:
             lab_copy.wait()
-            lab_all = lab_send[...] + pltpu.roll(lab_recv[...], 64, 1)
+            lab_all = [lab_send[0], lab_send[1], lab_recv[0], lab_recv[1]]
             gax[1, px] = gram_sum(0, gram)
             gram = gram_send(1)
         m_copy.wait()
-        margin = m_send[it] + pltpu.roll(m_recv[it], 64, 1)
-        resid = jax.nn.sigmoid(margin) - lab_all
         for k in range(4):
-            line = jnp.sum(turn * resid[:, k * 32:k * 32 + 1], axis=0, keepdims=True)
+            resid = jax.nn.sigmoid(m_send[it, (k + 2) % 4] + m_recv[it, k]) - lab_all[k]
+            line = jnp.sum(turn * resid, axis=0, keepdims=True)
             r_ref[:, k * 128:(k + 1) * 128] = jnp.where(on_diag, line, 0.0).astype(BF16)
 
         def scatter_send(batch):
@@ -306,6 +309,7 @@
             vectors.append(gp_ref)
             for t in range(16):
                 y_v[0:1, t * 128:(t + 1) * 128] = gp_ref[t:t + 1, :]
+        sums = jnp.zeros((m, 128), F32)
         for v, vec in enumerate(vectors):
             acc_s = jnp.zeros((m, 128), F32)
             acc_y = jnp.zeros((m, 128), F32)
@@ -313,11 +317,12 @@
                 line = vec[t:t + 1, :]
                 acc_s = acc_s + s_v[:, t * 128:(t + 1) * 128] * line
                 acc_y = acc_y + y_v[:, t * 128:(t + 1) * 128] * line
-            acc_ref[v * 64:v * 64 + m, :] = acc_s
-            acc_ref[v * 64 + 32:v * 64 + 32 + m, :] = acc_y
-        sums = contract_last(jnp.ones((8, 128), F32), acc_ref[...])
-        ar_own[it] = sums[0:1, :]
-        ar[it, chip * 2 + core] = sums[0:1, :]
+            for part, acc in ((2 * v, acc_s), (2 * v + 1, acc_y)):
+                own_lane = lane_m == row_m + 32 * part
+                sums = sums + jnp.where(own_lane, jnp.sum(acc, axis=1, keepdims=True), 0.0)
+        sums = jnp.sum(sums, axis=0, keepdims=True)
+        ar_own[it] = sums
+        ar[it, chip * 2 + core] = sums
 
         def total_send(device):
             pltpu.make_async_remote_copy(
@@ -330,6 +335,11 @@
             total_send((cy, cxz * 2))
             total_send((cy, cxz * 2 + 1))
         total_send(partner)
+        if it == 0:
+            def widen(c, carry):
+                x_f[c] = x_v[c].astype(F32)
+                return carry
+            lax.fori_loop(0, chips, widen, 0)
         whole(ar.at[it, pl.ds(0, 2 * chips - 1)], ar_rsem.at[it]).wait()
         tot = jnp.broadcast_to(jnp.sum(ar[it], axis=0), (8, 128))
         u, hh = tot[0:1], pltpu.roll(tot, 96, 1)[0:1]
@@ -400,6 +410,7 @@
         scratch_shapes=[
             pltpu.VMEM((chips, 4, 128, 128), BF16),
             pltpu.VMEM((chips, 2, 128, 128), BF16),
+            pltpu.VMEM((chips, 4, 128, 128), F32),
             pltpu.SMEM((16,), jnp.int32),
             pltpu.VMEM((16, 128), F32),
             pltpu.VMEM((m, 2048), F32),
@@ -414,12 +425,11 @@
             pltpu.VMEM((24, 128), F32),
             pltpu.VMEM((2, 24, 128), F32),
             pltpu.VMEM((3, 4, 24, 128), F32),
-            pltpu.VMEM((8, 128), F32),
-            pltpu.VMEM((8, 128), F32),
-            pltpu.VMEM((ITERS, 8, 128), F32),
-            pltpu.VMEM((ITERS, 8, 128), F32),
+            pltpu.VMEM((2, 8, 128), F32),
+            pltpu.VMEM((2, 8, 128), F32),
+            pltpu.VMEM((ITERS, 4, 8, 128), F32),
+            pltpu.VMEM((ITERS, 4, 8, 128), F32),
             pltpu.VMEM((16, 512), BF16),
-            pltpu.VMEM((128, 128), F32),
             pltpu.VMEM((128, 128), F32),
             pltpu.VMEM((16, 128), F32),
             pltpu.VMEM((16, 128), F32),

time: 57.2 us -> 56.5 us (0.988)
  Pallas kernels: 55.8 us -> 55.2 us
    pallas_call x1, Pallas kernels: 55.8 us -> 55.2 us  [per_device(): pl.pallas_call(functools.partial(kernel, sizes), out_shape=pltpu.VMEM((2,...]
where the time goes in v2:
time: 56.5 us; the launch traced here: 56.4 us
  Pallas kernels  55.2 us (98%)
  between operations  0.64 us (1%)
  local copies, waits for them, and re-layouts  0.61 us (1%)
    pallas_call x1, Pallas kernels, per_device(): pl.pallas_call(functools.partial(kernel, sizes), out_shape=pltpu.VMEM((2,...  55.2 us

profile of v2, /device:TPU:1, one launch (start us, length us, event | category | flops | bytes accessed | tf_op | source)
XLA Modules:
  0.0 56.4 jit_solution(15359680137325612370)
XLA Ops:
  0.6 55.2 %shard_map.68 = f32[2,16,128]{2,1,0:T(8,128)S(1)} custom-call(bf16[2,64,2,128,128]{4,3,2,1,0:T(8,128)(2,1)} %bitcast.10, s32[16]{0:T(128)} %lab_hbm.1, f32[16,128]{1,0:T(8,128)} %bitcast.11, f32[20,2048]{1,0:T(8,128)} %s_hbm.1, f32[20,2048]{1,0:T(8,128)} %y_hbm.1), custom_call_target="tpu_custom_call" | custom-call | tf_op jit(solution)/shard_map/pallas_call | solution.py:405
  55.8 0.6 %slice_bitcast_fusion = (f32[2048]{0:T(1024)}, f32[2048]{0:T(1024)}) fusion(f32[2,16,128]{2,1,0:T(8,128)S(1)} %shard_map.68), kind=kLoop, calls=%fused_computation | loop fusion | bytes 32768 | tf_op jit(solution)/shard_map/squeeze | solution.py:445

commit v3 on v2

--- a/solution.py
+++ b/solution.py
@@ -13,7 +13,7 @@
 HI = lax.Precision.HIGHEST
 F32 = jnp.float32
 BF16 = jnp.bfloat16
-BATCHES = (8, 8, 16, 16, 16)
+BATCHES = (8, 8, 8, 8, 8, 8, 8, 8)
 
 
 def contract_last(a, b):
@@ -28,8 +28,7 @@
     sizes, x_hbm, lab_hbm, w_hbm, s_hbm, y_hbm, out_ref,
     x_v, x_out, x_f, lab_ref, w_ref, s_v, y_v, w_own, wg, rs_send, rs_recv, ar_own, ar, gl, gtmp, gcore, gax,
     lab_send, lab_recv, m_send, m_recv, r_ref, t_ref, g_ref, gp_ref, d_ref,
-    x_sem, xr_send, xr_recv, h_sem, ag_send, ag_recv, rs_ssem, rs_rsem,
-    ar_ssem, ar_rsem, g_ssem, g_rsem, l_sem, m_ssem, m_rsem,
+    x_sem, xr_send, xr_recv, h_sem, ag_send, ag_recv, rs_sem, ar_sem, g_sem, l_sem, m_sem,
 ):
     ny, nx, nz = sizes
     plane = nx * nz
@@ -81,6 +80,9 @@
                 lows.append([places[1], places[0]])
         return [a + b + c for a in lows[0] for b in lows[1] for c in lows[2]]
 
+    def whole(ref, sem):
+        return pltpu.make_async_copy(ref, ref, sem)
+
     hist = [
         pltpu.make_async_copy(s_hbm, s_v, h_sem.at[0]),
         pltpu.make_async_copy(y_hbm, y_v, h_sem.at[1]),
@@ -91,16 +93,10 @@
     ]
     for copy in small + hist:
         copy.start()
-    local = []
     for h in range(2):
-        copy = pltpu.make_async_copy(x_hbm.at[h, :, other], x_v.at[:, h], x_sem.at[h])
-        copy.start()
-        local.append(copy)
-    staged = []
+        pltpu.make_async_copy(x_hbm.at[h, :, core], x_out.at[:, h], x_sem.at[1]).start()
     for h in range(2):
-        copy = pltpu.make_async_copy(x_hbm.at[h, :, core], x_out.at[:, h], x_sem.at[2 + h])
-        copy.start()
-        staged.append(copy)
+        pltpu.make_async_copy(x_hbm.at[h, :, other], x_v.at[:, h], x_sem.at[0]).start()
 
     barrier = pltpu.get_barrier_semaphore()
     for offset in offsets:
@@ -127,50 +123,44 @@
     gcore[core] = gl[...] + pltpu.roll(gtmp[...], 64, 1)
     pl.semaphore_wait(barrier, chips)
 
-    def whole(ref, sem):
-        return pltpu.make_async_copy(ref, ref, sem)
-
     def gather_start(it):
         for offset in offsets:
             pltpu.make_async_remote_copy(
                 src_ref=w_own.at[it], dst_ref=wg.at[it, chip],
-                send_sem=ag_send.at[it], recv_sem=ag_recv.at[it, round_of(offset)],
+                send_sem=ag_send.at[0], recv_sem=ag_recv.at[round_of(offset)],
                 device_id=dest(peer(offset)), device_id_type=MESH).start()
 
     gather_start(0)
 
     def gram_send(stage):
-        copies = []
         if stage == 3:
-            copies.append(pltpu.make_async_remote_copy(
+            pltpu.make_async_remote_copy(
                 src_ref=gcore.at[core], dst_ref=gcore.at[core],
-                send_sem=g_ssem.at[3, 0], recv_sem=g_rsem.at[3, 0],
-                device_id=partner, device_id_type=MESH))
-        else:
-            own = mine[stage]
-            for off in range(1, sizes[stage]):
-                offset = tuple(off if a == stage else 0 for a in range(3))
-                copies.append(pltpu.make_async_remote_copy(
-                    src_ref=gax.at[stage, own], dst_ref=gax.at[stage, own],
-                    send_sem=g_ssem.at[stage, off - 1], recv_sem=g_rsem.at[stage, off - 1],
-                    device_id=dest(peer(offset)), device_id_type=MESH))
-        for copy in copies:
-            copy.start()
-        return copies
-
-    def gram_sum(stage, copies):
-        for copy in copies:
-            copy.wait()
+                send_sem=g_sem.at[4], recv_sem=g_sem.at[3],
+                device_id=partner, device_id_type=MESH).start()
+            return
+        own = mine[stage]
+        for off in range(1, sizes[stage]):
+            offset = tuple(off if a == stage else 0 for a in range(3))
+            pltpu.make_async_remote_copy(
+                src_ref=gax.at[stage, own], dst_ref=gax.at[stage, own],
+                send_sem=g_sem.at[5 + stage], recv_sem=g_sem.at[stage],
+                device_id=dest(peer(offset)), device_id_type=MESH).start()
+
+    def gram_sum(stage):
         if stage == 3:
+            for i in (4, 3):
+                whole(gcore.at[0], g_sem.at[i]).wait()
             return gcore[0] + gcore[1]
+        for i in (5 + stage, stage):
+            whole(gax.at[stage, pl.ds(0, sizes[stage] - 1)], g_sem.at[i]).wait()
         total = gax[stage, 0]
         for place in range(1, sizes[stage]):
             total = total + gax[stage, place]
         return total
 
-    gram = gram_send(3)
-    for copy in staged:
-        copy.wait()
+    gram_send(3)
+    whole(x_out, x_sem.at[1]).wait()
     for offset in reversed(offsets):
         c = index(offset, behind)
         pltpu.make_async_remote_copy(
@@ -182,8 +172,8 @@
         device_id=partner, device_id_type=MESH)
     lab_copy.start()
 
-    gax[0, ex] = gram_sum(3, gram)
-    gram = gram_send(0)
+    gax[0, ex] = gram_sum(3)
+    gram_send(0)
 
     row16 = lax.broadcasted_iota(jnp.int32, (16, 128), 0)
     tile16 = lax.broadcasted_iota(jnp.int32, (16, 128), 1) // 8
@@ -227,35 +217,40 @@
     rinv = rinvt = yy = diag = gamma0 = None
     for it in range(ITERS):
         if it == 0:
-            for copy in local:
-                copy.wait()
+            whole(x_out, x_sem.at[0]).wait()
+
+        groups, per = rounds, 1
 
         def arrive(i, accs):
-            k = rounds - 1 - i
+            g = groups - 1 - i
             if it == 0:
-                whole(x_out.at[pl.ds(0, 8)], xr_recv.at[k]).wait()
-            whole(wg.at[it, pl.ds(0, 8)], ag_recv.at[it, k]).wait()
-            return margin_terms(it, round_blocks(k, behind), accs)
-
-        if it == 0:
-            accs = lax.fori_loop(0, rounds, arrive, zeros(6) + (jnp.zeros((16, 128), F32),))
+                whole(x_out.at[pl.ds(0, 8 * per)], xr_recv.at[g]).wait()
+            whole(wg.at[it, pl.ds(0, 8 * per)], ag_recv.at[g]).wait()
+            return lax.fori_loop(
+                0, per, lambda j, a: margin_terms(it, round_blocks(g * per + j, behind), a), accs)
+
+        if it == 0:
+            accs = arrive(0, zeros(6) + (jnp.zeros((16, 128), F32),))
+            gax[1, px] = gram_sum(0)
+            gram_send(1)
+            accs = lax.fori_loop(1, groups, arrive, accs)
             line = jnp.sum(jnp.where(on_diag, accs[6], 0.0), axis=0, keepdims=True)
             cols = lane_sums([accs[f] + accs[3 + f] for f in range(3)] + [turn * line])
         else:
-            accs = lax.fori_loop(0, rounds, arrive, zeros(8))
+            accs = lax.fori_loop(0, groups, arrive, zeros(8))
             cols = lane_sums([accs[f] + accs[4 + f] for f in range(4)])
         for k in range(4):
             m_send[it, (k + 2) % 4] = jnp.broadcast_to(cols[k], (8, 128))
         m_copy = pltpu.make_async_remote_copy(
             src_ref=m_send.at[it], dst_ref=m_recv.at[it],
-            send_sem=m_ssem.at[it], recv_sem=m_rsem.at[it],
+            send_sem=m_sem.at[0], recv_sem=m_sem.at[1],
             device_id=partner, device_id_type=MESH)
         m_copy.start()
+        if it > 0:
+            whole(ar.at[it - 1, pl.ds(0, 2 * chips - 1)], ar_sem.at[0]).wait()
         if it == 0:
             lab_copy.wait()
             lab_all = [lab_send[0], lab_send[1], lab_recv[0], lab_recv[1]]
-            gax[1, px] = gram_sum(0, gram)
-            gram = gram_send(1)
         m_copy.wait()
         for k in range(4):
             resid = jax.nn.sigmoid(m_send[it, (k + 2) % 4] + m_recv[it, k]) - lab_all[k]
@@ -266,12 +261,12 @@
             for offset in batch:
                 pltpu.make_async_remote_copy(
                     src_ref=rs_send.at[it, index(offset, ahead)], dst_ref=rs_recv.at[it, chip],
-                    send_sem=rs_ssem.at[it], recv_sem=rs_rsem.at[it],
+                    send_sem=rs_sem.at[0], recv_sem=rs_sem.at[1],
                     device_id=dest(peer(offset)), device_id_type=MESH).start()
 
         lines = r_ref[...]
         start = 0
-        for size in BATCHES:
+        for size in BATCHES[:1] if chips < 16 else BATCHES:
             batch = offsets[start:min(start + size, chips)]
             start += size
             for j in range(0, len(batch), 2):
@@ -281,10 +276,11 @@
                 rs_send[it, c0] = term[:, 0:128]
                 rs_send[it, c1] = term[:, 128:256]
             scatter_send(batch)
-        if it == 0:
-            gax[2, pz] = gram_sum(1, gram)
-            gram = gram_send(2)
-            total = gram_sum(2, gram)
+            if it == 0 and start == (BATCHES[0] if chips < 16 else sum(BATCHES[:2])):
+                gax[2, pz] = gram_sum(1)
+                gram_send(2)
+        if it == 0:
+            total = gram_sum(2)
             upper = jnp.where((row24 <= lane24) & (lane24 < m), total, 0.0)
             yy = jnp.where((lane24 < m) & (row24 < m), pltpu.roll(total, 64, 1), 0.0)
             diag = upper * eye
@@ -297,7 +293,8 @@
             t_ref[0:24, :] = inv
             rinvt = t_ref[...].T[0:24, :]
             gamma0 = upper[m - 1:m, m - 1:m] / yy[m - 1:m, m - 1:m]
-        whole(rs_recv.at[it], rs_rsem.at[it]).wait()
+        whole(wg.at[it], ag_send.at[0]).wait()
+        whole(rs_recv.at[it], rs_sem.at[1]).wait()
 
         def add(k, total):
             return total + rs_recv[it, k].astype(F32)
@@ -327,7 +324,7 @@
         def total_send(device):
             pltpu.make_async_remote_copy(
                 src_ref=ar_own.at[it], dst_ref=ar.at[it, chip * 2 + core],
-                send_sem=ar_ssem.at[it], recv_sem=ar_rsem.at[it],
+                send_sem=ar_sem.at[0], recv_sem=ar_sem.at[1],
                 device_id=device, device_id_type=MESH).start()
 
         for offset in offsets[:-1]:
@@ -340,7 +337,8 @@
                 x_f[c] = x_v[c].astype(F32)
                 return carry
             lax.fori_loop(0, chips, widen, 0)
-        whole(ar.at[it, pl.ds(0, 2 * chips - 1)], ar_rsem.at[it]).wait()
+        whole(rs_send.at[it], rs_sem.at[0]).wait()
+        whole(ar.at[it, pl.ds(0, 2 * chips - 1)], ar_sem.at[1]).wait()
         tot = jnp.broadcast_to(jnp.sum(ar[it], axis=0), (8, 128))
         u, hh = tot[0:1], pltpu.roll(tot, 96, 1)[0:1]
         if it == 0:
@@ -387,10 +385,7 @@
             out_ref[1] = direction
 
     whole(x_out, xr_send.at[0]).wait()
-    for it in range(ITERS):
-        whole(wg.at[it], ag_send.at[it]).wait()
-        whole(rs_send.at[it], rs_ssem.at[it]).wait()
-        whole(ar.at[it, pl.ds(0, 2 * chips - 1)], ar_ssem.at[it]).wait()
+    whole(ar.at[0, pl.ds(0, 2 * chips - 1)], ar_sem.at[0]).wait()
 
 
 def per_device(sizes, features, labels, start_weights, hist_s, hist_y):
@@ -434,10 +429,8 @@
             pltpu.VMEM((16, 128), F32),
             pltpu.VMEM((16, 128), F32),
             pltpu.VMEM((16, 128), F32),
-            dma((4,)), dma((1,)), dma((chips // 8,)), dma((4,)),
-            dma((ITERS,)), dma((ITERS, chips // 8)), dma((ITERS,)), dma((ITERS,)),
-            dma((ITERS,)), dma((ITERS,)),
-            dma((4, 3)), dma((4, 3)), dma((2,)), dma((ITERS,)), dma((ITERS,)),
+            dma((2,)), dma((1,)), dma((chips // 8,)), dma((4,)), dma((1,)), dma((chips // 8,)),
+            dma((2,)), dma((2,)), dma((8,)), dma((2,)), dma((2,)),
         ],
         compiler_params=pltpu.CompilerParams(collective_id=0, has_side_effects=True),
     )(x, labels, start_weights.reshape(16, 128), hist_s, hist_y)

time: 56.5 us -> 56.1 us (level)
  no operation moved by 1% of the time
where the time goes in v3:
time: 56.1 us; the launch traced here: 56 us
  Pallas kernels  54.7 us (98%)
  between operations  0.64 us (1%)
  local copies, waits for them, and re-layouts  0.61 us (1%)
    pallas_call x1, Pallas kernels, per_device(): pl.pallas_call(functools.partial(kernel, sizes), out_shape=pltpu.VMEM((2,...  54.7 us

profile of v3, /device:TPU:1, one launch (start us, length us, event | category | flops | bytes accessed | tf_op | source)
XLA Modules:
  0.0 56.0 jit_solution(15684379932620343702)
XLA Ops:
  0.6 54.7 %shard_map.68 = f32[2,16,128]{2,1,0:T(8,128)S(1)} custom-call(bf16[2,64,2,128,128]{4,3,2,1,0:T(8,128)(2,1)} %bitcast.10, s32[16]{0:T(128)} %lab_hbm.1, f32[16,128]{1,0:T(8,128)} %bitcast.11, f32[20,2048]{1,0:T(8,128)} %s_hbm.1, f32[20,2048]{1,0:T(8,128)} %y_hbm.1), custom_call_target="tpu_custom_call" | custom-call | tf_op jit(solution)/shard_map/pallas_call | solution.py:400
  55.3 0.6 %slice_bitcast_fusion = (f32[2048]{0:T(1024)}, f32[2048]{0:T(1024)}) fusion(f32[2,16,128]{2,1,0:T(8,128)S(1)} %shard_map.68), kind=kLoop, calls=%fused_computation | loop fusion | bytes 32768 | tf_op jit(solution)/shard_map/squeeze | solution.py:438

commit v4 on v3

--- a/solution.py
+++ b/solution.py
@@ -27,7 +27,7 @@
 def kernel(
     sizes, x_hbm, lab_hbm, w_hbm, s_hbm, y_hbm, out_ref,
     x_v, x_out, x_f, lab_ref, w_ref, s_v, y_v, w_own, wg, rs_send, rs_recv, ar_own, ar, gl, gtmp, gcore, gax,
-    lab_send, lab_recv, m_send, m_recv, r_ref, t_ref, g_ref, gp_ref, d_ref,
+    lab_send, lab_recv, m_send, m_recv, r_ref, t_ref, g_ref, gp_ref, d_ref, rs_f, data_ref,
     x_sem, xr_send, xr_recv, h_sem, ag_send, ag_recv, rs_sem, ar_sem, g_sem, l_sem, m_sem,
 ):
     ny, nx, nz = sizes
@@ -272,9 +272,13 @@
             for j in range(0, len(batch), 2):
                 c0, c1 = index(batch[j], ahead), index(batch[j + 1], ahead)
                 both = jnp.concatenate([x_v[c0].reshape(512, 128), x_v[c1].reshape(512, 128)], axis=1)
-                term = jnp.dot(lines, both, preferred_element_type=F32).astype(BF16)
-                rs_send[it, c0] = term[:, 0:128]
-                rs_send[it, c1] = term[:, 128:256]
+                term = jnp.dot(lines, both, preferred_element_type=F32)
+                for c, part in ((c0, term[:, 0:128]), (c1, term[:, 128:256])):
+                    if it == 0:
+                        rs_f[c] = part
+                    else:
+                        part = part - rs_f[c]
+                    rs_send[it, c] = part.astype(BF16)
             scatter_send(batch)
             if it == 0 and start == (BATCHES[0] if chips < 16 else sum(BATCHES[:2])):
                 gax[2, pz] = gram_sum(1)
@@ -298,7 +302,10 @@
 
         def add(k, total):
             return total + rs_recv[it, k].astype(F32)
-        grad = lax.fori_loop(0, chips, add, jnp.zeros((16, 128), F32), unroll=8) + 0.1 * weights
+        total = lax.fori_loop(0, chips, add, jnp.zeros((16, 128), F32) if it == 0 else data_ref[...], unroll=8)
+        if it == 0:
+            data_ref[...] = total
+        grad = total + 0.1 * weights
         g_ref[...] = grad
         vectors = [g_ref]
         if it > 0:
@@ -429,6 +436,8 @@
             pltpu.VMEM((16, 128), F32),
             pltpu.VMEM((16, 128), F32),
             pltpu.VMEM((16, 128), F32),
+            pltpu.VMEM((chips, 16, 128), F32),
+            pltpu.VMEM((16, 128), F32),
             dma((2,)), dma((1,)), dma((chips // 8,)), dma((4,)), dma((1,)), dma((chips // 8,)),
             dma((2,)), dma((2,)), dma((8,)), dma((2,)), dma((2,)),
         ],

time: 56.1 us -> 56.1 us (level)
  no operation moved by 1% of the time
where the time goes in v4:
time: 56.1 us; the launch traced here: 56 us
  Pallas kernels  54.7 us (98%)
  between operations  0.64 us (1%)
  local copies, waits for them, and re-layouts  0.61 us (1%)
    pallas_call x1, Pallas kernels, per_device(): pl.pallas_call(functools.partial(kernel, sizes), out_shape=pltpu.VMEM((2,...  54.7 us

profile of v4, /device:TPU:1, one launch (start us, length us, event | category | flops | bytes accessed | tf_op | source)
XLA Modules:
  0.0 56.0 jit_solution(12527170618225775898)
XLA Ops:
  0.6 54.7 %shard_map.68 = f32[2,16,128]{2,1,0:T(8,128)S(1)} custom-call(bf16[2,64,2,128,128]{4,3,2,1,0:T(8,128)(2,1)} %bitcast.10, s32[16]{0:T(128)} %lab_hbm.1, f32[16,128]{1,0:T(8,128)} %bitcast.11, f32[20,2048]{1,0:T(8,128)} %s_hbm.1, f32[20,2048]{1,0:T(8,128)} %y_hbm.1), custom_call_target="tpu_custom_call" | custom-call | tf_op jit(solution)/shard_map/pallas_call | solution.py:407
  55.4 0.6 %slice_bitcast_fusion = (f32[2048]{0:T(1024)}, f32[2048]{0:T(1024)}) fusion(f32[2,16,128]{2,1,0:T(8,128)S(1)} %shard_map.68), kind=kLoop, calls=%fused_computation | loop fusion | bytes 32768 | tf_op jit(solution)/shard_map/squeeze | solution.py:447

commit v5 on v4

--- a/solution.py
+++ b/solution.py
@@ -27,7 +27,7 @@
 def kernel(
     sizes, x_hbm, lab_hbm, w_hbm, s_hbm, y_hbm, out_ref,
     x_v, x_out, x_f, lab_ref, w_ref, s_v, y_v, w_own, wg, rs_send, rs_recv, ar_own, ar, gl, gtmp, gcore, gax,
-    lab_send, lab_recv, m_send, m_recv, r_ref, t_ref, g_ref, gp_ref, d_ref, rs_f, data_ref,
+    lab_send, lab_recv, m_send, m_recv, r_ref, t_ref, g_ref, gp_ref, d_ref, data_ref,
     x_sem, xr_send, xr_recv, h_sem, ag_send, ag_recv, rs_sem, ar_sem, g_sem, l_sem, m_sem,
 ):
     ny, nx, nz = sizes
@@ -274,10 +274,8 @@
                 both = jnp.concatenate([x_v[c0].reshape(512, 128), x_v[c1].reshape(512, 128)], axis=1)
                 term = jnp.dot(lines, both, preferred_element_type=F32)
                 for c, part in ((c0, term[:, 0:128]), (c1, term[:, 128:256])):
-                    if it == 0:
-                        rs_f[c] = part
-                    else:
-                        part = part - rs_f[c]
+                    if it > 0:
+                        part = part - rs_send[it - 1, c].astype(F32)
                     rs_send[it, c] = part.astype(BF16)
             scatter_send(batch)
             if it == 0 and start == (BATCHES[0] if chips < 16 else sum(BATCHES[:2])):
@@ -436,7 +434,6 @@
             pltpu.VMEM((16, 128), F32),
             pltpu.VMEM((16, 128), F32),
             pltpu.VMEM((16, 128), F32),
-            pltpu.VMEM((chips, 16, 128), F32),
             pltpu.VMEM((16, 128), F32),
             dma((2,)), dma((1,)), dma((chips // 8,)), dma((4,)), dma((1,)), dma((chips // 8,)),
             dma((2,)), dma((2,)), dma((8,)), dma((2,)), dma((2,)),

time: 56.1 us -> 56.4 us (level)
  no operation moved by 1% of the time
where the time goes in v5:
time: 56.4 us; the launch traced here: 56.3 us
  Pallas kernels  55 us (98%)
  between operations  0.64 us (1%)
  local copies, waits for them, and re-layouts  0.61 us (1%)
    pallas_call x1, Pallas kernels, per_device(): pl.pallas_call(functools.partial(kernel, sizes), out_shape=pltpu.VMEM((2,...  55 us

profile of v5, /device:TPU:1, one launch (start us, length us, event | category | flops | bytes accessed | tf_op | source)
XLA Modules:
  0.0 56.3 jit_solution(18026230641268140858)
XLA Ops:
  0.6 55.0 %shard_map.68 = f32[2,16,128]{2,1,0:T(8,128)S(1)} custom-call(bf16[2,64,2,128,128]{4,3,2,1,0:T(8,128)(2,1)} %bitcast.10, s32[16]{0:T(128)} %lab_hbm.1, f32[16,128]{1,0:T(8,128)} %bitcast.11, f32[20,2048]{1,0:T(8,128)} %s_hbm.1, f32[20,2048]{1,0:T(8,128)} %y_hbm.1), custom_call_target="tpu_custom_call" | custom-call | tf_op jit(solution)/shard_map/pallas_call | solution.py:405
  55.7 0.6 %slice_bitcast_fusion = (f32[2048]{0:T(1024)}, f32[2048]{0:T(1024)}) fusion(f32[2,16,128]{2,1,0:T(8,128)S(1)} %shard_map.68), kind=kLoop, calls=%fused_computation | loop fusion | bytes 32768 | tf_op jit(solution)/shard_map/squeeze | solution.py:444

commit v6 on v3

--- a/solution.py
+++ b/solution.py
@@ -13,7 +13,7 @@
 HI = lax.Precision.HIGHEST
 F32 = jnp.float32
 BF16 = jnp.bfloat16
-BATCHES = (8, 8, 8, 8, 8, 8, 8, 8)
+BATCHES = (4, 4, 8, 8, 8, 8, 8, 8, 8)
 
 
 def contract_last(a, b):
@@ -266,7 +266,7 @@
 
         lines = r_ref[...]
         start = 0
-        for size in BATCHES[:1] if chips < 16 else BATCHES:
+        for size in BATCHES[:2] if chips < 16 else BATCHES:
             batch = offsets[start:min(start + size, chips)]
             start += size
             for j in range(0, len(batch), 2):
@@ -276,7 +276,7 @@
                 rs_send[it, c0] = term[:, 0:128]
                 rs_send[it, c1] = term[:, 128:256]
             scatter_send(batch)
-            if it == 0 and start == (BATCHES[0] if chips < 16 else sum(BATCHES[:2])):
+            if it == 0 and start == (8 if chips < 16 else sum(BATCHES[:3])):
                 gax[2, pz] = gram_sum(1)
                 gram_send(2)
         if it == 0:
@@ -292,7 +292,7 @@
             rinv = inv
             t_ref[0:24, :] = inv
             rinvt = t_ref[...].T[0:24, :]
-            gamma0 = upper[m - 1:m, m - 1:m] / yy[m - 1:m, m - 1:m]
+            gamma0 = jnp.broadcast_to(upper[m - 1:m, m - 1:m] / yy[m - 1:m, m - 1:m], (24, 128))
         whole(wg.at[it], ag_send.at[0]).wait()
         whole(rs_recv.at[it], rs_sem.at[1]).wait()
 
@@ -344,13 +344,13 @@
         if it == 0:
             gamma = gamma0
             alpha = -jnp.sum(rinv * u, axis=1, keepdims=True)
-            p = gamma * (jnp.sum(yy * alpha, axis=0, keepdims=True) + hh)
+            p = gamma[0:1] * (jnp.sum(yy * alpha, axis=0, keepdims=True) + hh)
             p = p + jnp.sum(diag * alpha, axis=0, keepdims=True)
             coef = jnp.sum(rinvt * p, axis=1, keepdims=True)
         else:
             v, z = pltpu.roll(tot, 64, 1)[0:1], pltpu.roll(tot, 32, 1)[0:1]
             v0, z0, u0 = v[:, 0:1], z[:, 0:1], u[:, 0:1]
-            gamma = v0 / z0
+            gamma = jnp.broadcast_to(v0 / z0, (24, 128))
             a0 = -u0 / v0
             old = (row24 > 0) & (lane24 > 0)
             rm, rmt = jnp.where(old, rinv, 0.0), jnp.where(old, rinvt, 0.0)
@@ -361,16 +361,16 @@
             flat = jnp.sum(eye * alpha, axis=0, keepdims=True)
             newest = jnp.sum(jnp.where(lane1 < m, z, 0.0) * flat, axis=1, keepdims=True)
             q = jnp.sum(jnp.where(old, yy, 0.0) * alpha, axis=0, keepdims=True) + z * a0
-            p = gamma * (q + hh) + jnp.sum(diag * alpha, axis=0, keepdims=True)
+            p = gamma[0:1] * (q + hh) + jnp.sum(diag * alpha, axis=0, keepdims=True)
             coef = jnp.sum(rmt * p, axis=1, keepdims=True)
             rest = jnp.sum(rv_flat * p, axis=1, keepdims=True)
-            c0 = (gamma * (newest + hh[:, 0:1]) + v0 * a0 - rest) / v0
+            c0 = (gamma[0:1, 0:1] * (newest + hh[:, 0:1]) + v0 * a0 - rest) / v0
             coef = jnp.where(row24[:, 0:1] == 0, c0, coef)
         cs, cy = coef[0:m], (-gamma * alpha)[0:m]
         for t in range(16):
             cols = slice(t * 128, (t + 1) * 128)
             d_ref[t:t + 1, :] = jnp.sum(cs * s_v[:, cols] + cy * y_v[:, cols], axis=0, keepdims=True)
-        direction = d_ref[...] - gamma * g_ref[...]
+        direction = d_ref[...] - gamma[0:16] * g_ref[...]
         new = weights + direction
         if it < ITERS - 1:
             w_own[it + 1] = new.astype(BF16)

time: 56.1 us -> 56.2 us (level)
  no operation moved by 1% of the time
where the time goes in v6:
time: 56.2 us; the launch traced here: 56.1 us
  Pallas kernels  54.8 us (98%)
  between operations  0.64 us (1%)
  local copies, waits for them, and re-layouts  0.61 us (1%)
    pallas_call x1, Pallas kernels, per_device(): pl.pallas_call(functools.partial(kernel, sizes), out_shape=pltpu.VMEM((2,...  54.8 us

profile of v6, /device:TPU:1, one launch (start us, length us, event | category | flops | bytes accessed | tf_op | source)
XLA Modules:
  0.0 56.1 jit_solution(6108222902839348341)
XLA Ops:
  0.6 54.8 %shard_map.68 = f32[2,16,128]{2,1,0:T(8,128)S(1)} custom-call(bf16[2,64,2,128,128]{4,3,2,1,0:T(8,128)(2,1)} %bitcast.10, s32[16]{0:T(128)} %lab_hbm.1, f32[16,128]{1,0:T(8,128)} %bitcast.11, f32[20,2048]{1,0:T(8,128)} %s_hbm.1, f32[20,2048]{1,0:T(8,128)} %y_hbm.1), custom_call_target="tpu_custom_call" | custom-call | tf_op jit(solution)/shard_map/pallas_call | solution.py:400
  55.5 0.6 %slice_bitcast_fusion = (f32[2048]{0:T(1024)}, f32[2048]{0:T(1024)}) fusion(f32[2,16,128]{2,1,0:T(8,128)S(1)} %shard_map.68), kind=kLoop, calls=%fused_computation | loop fusion | bytes 32768 | tf_op jit(solution)/shard_map/squeeze | solution.py:438

commit v7 on v6

--- a/solution.py
+++ b/solution.py
@@ -13,7 +13,7 @@
 HI = lax.Precision.HIGHEST
 F32 = jnp.float32
 BF16 = jnp.bfloat16
-BATCHES = (4, 4, 8, 8, 8, 8, 8, 8, 8)
+BATCHES = (8, 8, 8, 8, 8, 8, 8, 8)
 
 
 def contract_last(a, b):
@@ -266,7 +266,7 @@
 
         lines = r_ref[...]
         start = 0
-        for size in BATCHES[:2] if chips < 16 else BATCHES:
+        for size in BATCHES[:1] if chips < 16 else BATCHES:
             batch = offsets[start:min(start + size, chips)]
             start += size
             for j in range(0, len(batch), 2):
@@ -276,7 +276,7 @@
                 rs_send[it, c0] = term[:, 0:128]
                 rs_send[it, c1] = term[:, 128:256]
             scatter_send(batch)
-            if it == 0 and start == (8 if chips < 16 else sum(BATCHES[:3])):
+            if it == 0 and start == (BATCHES[0] if chips < 16 else sum(BATCHES[:2])):
                 gax[2, pz] = gram_sum(1)
                 gram_send(2)
         if it == 0:

time: 56.2 us -> 56.1 us (level)
  no operation moved by 1% of the time
where the time goes in v7:
time: 56.1 us; the launch traced here: 55.9 us
  Pallas kernels  54.7 us (98%)
  between operations  0.64 us (1%)
  local copies, waits for them, and re-layouts  0.61 us (1%)
    pallas_call x1, Pallas kernels, per_device(): pl.pallas_call(functools.partial(kernel, sizes), out_shape=pltpu.VMEM((2,...  54.7 us

profile of v7, /device:TPU:1, one launch (start us, length us, event | category | flops | bytes accessed | tf_op | source)
XLA Modules:
  0.0 55.9 jit_solution(4403416635892183408)
XLA Ops:
  0.6 54.7 %shard_map.68 = f32[2,16,128]{2,1,0:T(8,128)S(1)} custom-call(bf16[2,64,2,128,128]{4,3,2,1,0:T(8,128)(2,1)} %bitcast.10, s32[16]{0:T(128)} %lab_hbm.1, f32[16,128]{1,0:T(8,128)} %bitcast.11, f32[20,2048]{1,0:T(8,128)} %s_hbm.1, f32[20,2048]{1,0:T(8,128)} %y_hbm.1), custom_call_target="tpu_custom_call" | custom-call | tf_op jit(solution)/shard_map/pallas_call | solution.py:400
  55.3 0.6 %slice_bitcast_fusion = (f32[2048]{0:T(1024)}, f32[2048]{0:T(1024)}) fusion(f32[2,16,128]{2,1,0:T(8,128)S(1)} %shard_map.68), kind=kLoop, calls=%fused_computation | loop fusion | bytes 32768 | tf_op jit(solution)/shard_map/squeeze | solution.py:438
